TPU v7x, 32 devices: a whole 2x2x4 slice. The times are simulated.
32 devices in a mesh: gx: 4 (over y, core), gy: 4 (over z), gz: 2 (over x).
Axes of the slice: x: 2, y: 2, z: 4, core: 2. Of those that a mesh axis runs over, the one named last changes fastest.
Arguments:
- moments: float32 [8, 16, 64, 1024], P(None, 'gx', 'gy', 'gz'), may hold values from 0.001 to 60, as said below
- velocity: float32 [3, 16, 64, 1024], P(None, 'gx', 'gy', 'gz'), may hold values from -4 to 4
- drift: float32 [3, 16, 64, 1024], P(None, 'gx', 'gy', 'gz'), may hold values from -8 to 8
Outputs:
- updated: float32 [8, 16, 64, 1024], P(None, 'gx', 'gy', 'gz')
- totals: float32 [8], replicated
Inputs may be any that keep to these rules, and one draw needn't show every extreme that they name: In every cell the 8 entries are the moments of order 0 to 7 of a log-normal distribution of particle size.
All inputs are finite; a program needn't handle non-finite values. Where the computation divides by a largest or mean magnitude, that divisor is 1e-20 or more.
Results may differ from a plain program's by a relative error of at most 0.0003.
Values sent between devices are 32-bit elements; how exact they have to be, the bound alone decides.
A program may use at most 64 MiB of HBM per device.

v0:
```python
import functools

import jax
import jax.numpy as jnp
from jax import lax
from jax.experimental import pallas as pl
from jax.experimental.pallas import tpu as pltpu
from jax.sharding import PartitionSpec as P

SWEEPS = 6
AXES = ("gx", "gy", "gz")
JACOBI_LANES = 512
LANES = 128

cfl_number = 0.4
speed_eps = 1e-06
pair_list = ((0, 1), (0, 2), (0, 3), (1, 2), (1, 3), (2, 3))


def entry_key(i, j):
    return (min(i, j), max(i, j))


def rotated(cosine, sine, near, far):
    if near is None and far is None:
        return None, None
    if near is None:
        return -(sine * far), cosine * far
    if far is None:
        return cosine * near, sine * near
    return cosine * near - sine * far, sine * near + cosine * far


def invert(moment):
    levels = list(moment)
    before = None
    inverse = 1.0 / levels[0]
    ratios = [levels[1] * inverse]
    alphas = [ratios[0]]
    betas = [levels[0]]
    for level in range(1, 4):
        fresh = [None] * 8
        for column in range(level, 8 - level):
            value = levels[column + 1] - alphas[level - 1] * levels[column]
            if level > 1:
                value = value - betas[level - 1] * before[column]
            fresh[column] = value
        betas.append(fresh[level] * inverse)
        inverse = 1.0 / fresh[level]
        ratios.append(fresh[level + 1] * inverse)
        alphas.append(ratios[level] - ratios[level - 1])
        before, levels = levels, fresh
    table = {(i, j): None for i in range(4) for j in range(i, 4)}
    for i in range(4):
        table[i, i] = alphas[i]
    for i in range(3):
        table[i, i + 1] = jnp.sqrt(betas[i + 1])
    first = [1.0, None, None, None]
    for _ in range(SWEEPS):
        for p, q in pair_list:
            coupling = table[p, q]
            if coupling is None:
                continue
            spread = table[q, q] - table[p, p]
            double = coupling + coupling
            r = lax.rsqrt(spread * spread + double * double)
            c2 = 0.5 + 0.5 * (jnp.abs(spread) * r)
            rc = lax.rsqrt(c2)
            cosine = c2 * rc
            signed = jnp.where(spread >= 0, coupling, -coupling)
            sine = signed * (r * rc)
            shift = sine * rc * coupling
            for rest in range(4):
                if rest not in (p, q):
                    a, b = entry_key(rest, p), entry_key(rest, q)
                    table[a], table[b] = rotated(cosine, sine, table[a], table[b])
            table[p, p] = table[p, p] - shift
            table[q, q] = table[q, q] + shift
            table[p, q] = None
            first[p], first[q] = rotated(cosine, sine, first[p], first[q])
    weights = [moment[0] * first[i] * first[i] for i in range(4)]
    return weights, [table[i, i] for i in range(4)]


def outflow(weights, sizes, mean_speed, mean_drift, upwind):
    sums = None
    for w, s in zip(weights, sizes):
        term = w * upwind(mean_speed + mean_drift * s, 0.0)
        terms = [term]
        for _ in range(7):
            term = term * s
            terms.append(term)
        sums = terms if sums is None else [a + b for a, b in zip(sums, terms)]
    return sums


def kernel(
    sizes, m_hbm, v_hbm, g_hbm, out, tot_ref,
    m, v, g, nodes, acc, fx, zp, zm,
    hvx, vy_s, vy_r, vz_s, vz_r, y_s, y_r, z_s, z_r, peak, total,
    in_sem, nb_send, nb_recv, all_send, all_recv,
):
    X, Y, Z = m.shape[1:]
    count = sizes[0] * sizes[1] * sizes[2]
    at = [lax.axis_index(a) for a in AXES]
    me = (at[0] * sizes[1] + at[1]) * sizes[2] + at[2]
    row = lax.broadcasted_iota(jnp.int32, (Y, LANES), 0)
    lane = lax.broadcasted_iota(jnp.int32, (Y, LANES), 1)
    bottom = at[2] == 0
    top = at[2] == sizes[2] - 1

    def peer(offset):
        where = lax.rem(me + offset, count)
        return (
            where // (sizes[1] * sizes[2]),
            lax.rem(where // sizes[2], sizes[1]),
            lax.rem(where, sizes[2]),
        )

    def beside(axis, step):
        place = list(at)
        place[axis] = lax.rem(at[axis] + step + sizes[axis], sizes[axis])
        return tuple(place)

    loads = [pltpu.make_async_copy(m_hbm.at[:, x], m.at[:, x], in_sem.at[x]) for x in range(X)]
    loads_v = pltpu.make_async_copy(v_hbm, v, in_sem.at[X])
    loads_g = pltpu.make_async_copy(g_hbm, g, in_sem.at[X + 1])
    edge = [0] if X == 1 else [0, X - 1]
    inner = list(range(1, X - 1))
    loads[0].start()
    loads_v.start()
    loads_g.start()
    for x in edge[1:] + inner:
        loads[x].start()

    barrier = pltpu.get_barrier_semaphore()

    def greet(offset, carry):
        pl.semaphore_signal(
            barrier, inc=1, device_id=peer(offset), device_id_type=pl.DeviceIdType.MESH
        )
        return carry

    lax.fori_loop(1, count, greet, 0)

    sent = []

    def send(src, dst, axis, step):
        index = len(sent)
        copy = pltpu.make_async_remote_copy(
            src_ref=src, dst_ref=dst, send_sem=nb_send.at[index], recv_sem=nb_recv.at[index],
            device_id=beside(axis, step), device_id_type=pl.DeviceIdType.MESH,
        )
        copy.start()
        sent.append(copy)
        return copy

    loads_v.wait()
    loads_g.wait()
    for x in range(X):
        for part, ref in ((0, v), (1, g)):
            vy_s[0, x, part : part + 1, :] = ref[1, x, Y - 1 : Y, :]
            vy_s[1, x, part : part + 1, :] = ref[1, x, 0:1, :]
        high = [ref[2, x, :, Z - LANES : Z] for ref in (v, g)]
        low = [ref[2, x, :, 0:LANES] for ref in (v, g)]
        vz_s[0, x] = jnp.where(lane == 0, pltpu.roll(high[0], 1, 1), pltpu.roll(high[1], 2, 1))
        vz_s[1, x] = jnp.where(lane == 0, low[0], pltpu.roll(low[1], 1, 1))

    chunks = Z // JACOBI_LANES

    def solve(x, chunk, best):
        zs = pl.ds(pl.multiple_of(chunk * JACOBI_LANES, JACOBI_LANES), JACOBI_LANES)
        weights, places = invert([m[k, x, :, zs] for k in range(8)])
        for i in range(4):
            nodes[x + 1, i, :, zs] = weights[i]
            nodes[x + 1, 4 + i, :, zs] = places[i]
        speed = None
        for d in range(3):
            vd, gd = v[d, x, :, zs], g[d, x, :, zs]
            parts = [jnp.abs(vd + gd * s) for s in places]
            largest = jnp.maximum(
                jnp.maximum(parts[0], parts[1]), jnp.maximum(parts[2], parts[3])
            )
            speed = largest if speed is None else speed + largest
        return jnp.maximum(best, speed)

    best = jnp.zeros((Y, JACOBI_LANES), jnp.float32)
    def solve_layer(x, best):
        return lax.fori_loop(0, chunks, lambda i, b: solve(x, i, b), best)

    loads[0].wait()
    best = solve_layer(0, best)
    pl.semaphore_wait(barrier, count - 1)
    velocity_copies = [
        send(v.at[0, X - 1], hvx.at[0, 0], 0, 1),
        send(g.at[0, X - 1], hvx.at[0, 1], 0, 1),
        send(v.at[0, 0], hvx.at[1, 0], 0, -1),
        send(g.at[0, 0], hvx.at[1, 1], 0, -1),
        send(vy_s.at[0], vy_r.at[0], 1, 1),
        send(vy_s.at[1], vy_r.at[1], 1, -1),
        send(vz_s.at[0], vz_r.at[0], 2, 1),
        send(vz_s.at[1], vz_r.at[1], 2, -1),
    ]
    if X > 1:
        loads[X - 1].wait()
        best = solve_layer(X - 1, best)
    x_copies = [
        send(nodes.at[1], nodes.at[X + 1], 0, -1),
        send(nodes.at[X], nodes.at[0], 0, 1),
    ]

    def lanes_of(chunk):
        return pl.ds(pl.multiple_of(chunk * LANES, LANES), LANES)

    def nodes_of(layer, zs):
        return (
            [nodes[layer, i, :, zs] for i in range(4)],
            [nodes[layer, 4 + i, :, zs] for i in range(4)],
        )

    for x in inner:
        loads[x].wait()
    if inner:
        best = lax.fori_loop(
            0, len(inner) * chunks,
            lambda i, b: solve(lax.div(i, chunks) + 1, lax.rem(i, chunks), b), best,
        )

    best = jnp.max(best, axis=0, keepdims=True)
    best = functools.reduce(
        jnp.maximum, [best[:, i : i + LANES] for i in range(0, JACOBI_LANES, LANES)]
    )
    peak[0] = best

    def spread_copy(buffer, which, offset):
        return pltpu.make_async_remote_copy(
            src_ref=buffer.at[0], dst_ref=buffer.at[offset],
            send_sem=all_send.at[which, offset], recv_sem=all_recv.at[which, offset],
            device_id=peer(offset), device_id_type=pl.DeviceIdType.MESH,
        )

    def spread(buffer, which):
        def one(offset, carry):
            spread_copy(buffer, which, offset).start()
            return carry

        lax.fori_loop(1, count, one, 0)

    def gathered(buffer, which):
        def one(offset, carry):
            spread_copy(buffer, which, offset).wait_recv()
            return carry

        lax.fori_loop(1, count, one, 0)

    for copy in velocity_copies[4:]:
        copy.wait_recv()

    zc = Z // LANES

    def side_faces(i, carry):
        x, chunk = lax.div(i, zc), lax.rem(i, zc)
        zs = lanes_of(chunk)
        w, s = nodes_of(x + 1, zs)
        vy, gy = v[1, x, :, zs], g[1, x, :, zs]
        up = [
            jnp.where(row == Y - 1, vy_r[1, x, part : part + 1, zs], pltpu.roll(a, Y - 1, 0))
            for part, a in ((0, vy), (1, gy))
        ]
        down = [
            jnp.where(row == 0, vy_r[0, x, part : part + 1, zs], pltpu.roll(a, 1, 0))
            for part, a in ((0, vy), (1, gy))
        ]
        high = outflow(w, s, 0.5 * (vy + up[0]), 0.5 * (gy + up[1]), jnp.maximum)
        for k in range(8):
            y_s[0, x, k : k + 1, zs] = high[k][Y - 1 : Y, :]
            acc[x, k, :, zs] = high[k] - jnp.where(row == 0, 0.0, pltpu.roll(high[k], 1, 0))
        low = outflow(w, s, 0.5 * (vy + down[0]), 0.5 * (gy + down[1]), jnp.minimum)
        for k in range(8):
            y_s[1, x, k : k + 1, zs] = low[k][0:1, :]
            acc[x, k, :, zs] += (
                jnp.where(row == Y - 1, 0.0, pltpu.roll(low[k], Y - 1, 0)) - low[k]
            )
        return carry

    lax.fori_loop(0, X * zc, side_faces, 0)
    spread(peak, 0)
    y_copies = [send(y_s.at[0], y_r.at[0], 1, 1), send(y_s.at[1], y_r.at[1], 1, -1)]

    def wall_faces(i, carry):
        x, chunk = lax.div(i, zc), lax.rem(i, zc)
        zs = lanes_of(chunk)
        nxt = lanes_of(lax.rem(chunk + 1, zc))
        prv = lanes_of(lax.rem(chunk + zc - 1, zc))
        w, s = nodes_of(x + 1, zs)
        final = chunk == zc - 1
        start = chunk == 0

        def means(ref, part):
            here = ref[2, x, :, zs]
            after = jnp.where(final, pltpu.roll(vz_r[1, x], LANES - part, 1), ref[2, x, :, nxt])
            ahead = jnp.where(
                start, pltpu.roll(vz_r[0, x], LANES - 1 - part, 1), ref[2, x, :, prv]
            )
            up = jnp.where(
                lane == LANES - 1, pltpu.roll(after, LANES - 1, 1), pltpu.roll(here, LANES - 1, 1)
            )
            down = jnp.where(lane == 0, pltpu.roll(ahead, 1, 1), pltpu.roll(here, 1, 1))
            return 0.5 * (here + up), 0.5 * (here + down)

        speeds, slopes = means(v, 0), means(g, 1)
        shut_high = (lane == LANES - 1) & (final & top)
        shut_low = (lane == 0) & (start & bottom)
        high = outflow(w, s, speeds[0], slopes[0], jnp.maximum)
        for k in range(8):
            zp[x, k, :, zs] = jnp.where(shut_high, 0.0, high[k])
        low = outflow(w, s, speeds[1], slopes[1], jnp.minimum)
        for k in range(8):
            zm[x, k, :, zs] = jnp.where(shut_low, 0.0, low[k])
        return carry

    lax.fori_loop(0, X * zc, wall_faces, 0)

    def pack_z(x, carry):
        high = jnp.zeros((Y, LANES), jnp.float32)
        low = jnp.zeros((Y, LANES), jnp.float32)
        for k in range(8):
            high = jnp.where(
                lane == k, pltpu.roll(zp[x, k, :, Z - LANES : Z], k + 1, 1), high
            )
            column = zm[x, k, :, 0:LANES]
            low = jnp.where(lane == k, pltpu.roll(column, k, 1) if k else column, low)
        z_s[0, x] = high
        z_s[1, x] = low
        return carry

    lax.fori_loop(0, X, pack_z, 0)

    def face_x(face, zs, left, right):
        speed, slope = 0.5 * (left[0] + right[0]), 0.5 * (left[1] + right[1])
        upper = outflow(*nodes_of(face, zs), speed, slope, jnp.maximum)
        lower = outflow(*nodes_of(face + 1, zs), speed, slope, jnp.minimum)
        for k in range(8):
            fx[face, k, :, zs] = upper[k] + lower[k]

    def drift_of(x, zs):
        return v[0, x, :, zs], g[0, x, :, zs]

    def inner_x(i, carry):
        face, zs = lax.div(i, zc) + 1, lanes_of(lax.rem(i, zc))
        face_x(face, zs, drift_of(face - 1, zs), drift_of(face, zs))
        return carry

    def outer_x(i, carry):
        zs = lanes_of(i)
        face_x(0, zs, (hvx[0, 0, :, zs], hvx[0, 1, :, zs]), drift_of(0, zs))
        face_x(X, zs, drift_of(X - 1, zs), (hvx[1, 0, :, zs], hvx[1, 1, :, zs]))
        return carry

    z_copies = [send(z_s.at[0], z_r.at[0], 2, 1), send(z_s.at[1], z_r.at[1], 2, -1)]
    if X > 1:
        lax.fori_loop(0, (X - 1) * zc, inner_x, 0)

    for copy in velocity_copies[:4] + x_copies:
        copy.wait_recv()
    lax.fori_loop(0, zc, outer_x, 0)
    for copy in y_copies + z_copies:
        copy.wait_recv()

    wide_row = lax.broadcasted_iota(jnp.int32, (Y, Z), 0)
    wide_lane = lax.broadcasted_iota(jnp.int32, (Y, Z), 1)

    def fold(value):
        value = functools.reduce(jnp.add, [value[i : i + 8, :] for i in range(0, Y, 8)])
        return functools.reduce(jnp.add, [value[:, i : i + LANES] for i in range(0, Z, LANES)])

    def combine(x, sums):
        fresh = []
        low_all, high_all = z_r[0, x], z_r[1, x]
        for k in range(8):
            fp, fm = zp[x, k], zm[x, k]
            first = pltpu.roll(low_all, LANES - k, 1) if k else low_all
            last = pltpu.roll(high_all, LANES - 1 - k, 1)
            spare = [first] * (Z // LANES - 1)
            before = jnp.where(
                wide_lane == 0, jnp.concatenate([first] + spare, 1), pltpu.roll(fp, 1, 1)
            )
            spare = [last] * (Z // LANES - 1)
            after = jnp.where(
                wide_lane == Z - 1, jnp.concatenate(spare + [last], 1), pltpu.roll(fm, Z - 1, 1)
            )
            change = acc[x, k] + ((fp + after) - (fm + before))
            change = change + (fx[x + 1, k] - fx[x, k])
            change = change + jnp.where(
                wide_row == Y - 1, y_r[1, x, k : k + 1, :],
                jnp.where(wide_row == 0, -y_r[0, x, k : k + 1, :], 0.0),
            )
            acc[x, k] = change
            fresh.append(sums[k] + fold(m[k, x]))
            fresh.append(sums[8 + k] + fold(change))
        return tuple(fresh[0::2] + fresh[1::2])

    zero = jnp.zeros((8, LANES), jnp.float32)
    sums = lax.fori_loop(0, X, combine, (zero,) * 16)

    one_lane = lax.broadcasted_iota(jnp.int32, (1, LANES), 1)
    packed = jnp.zeros((1, LANES), jnp.float32)
    for k in range(16):
        value = jnp.sum(jnp.sum(sums[k], axis=0, keepdims=True), axis=1, keepdims=True)
        packed = jnp.where(one_lane == k, value, packed)
    total[0] = packed
    spread(total, 1)
    gathered(peak, 0)
    largest = jnp.max(jnp.max(peak[...], axis=0), axis=1, keepdims=True)
    step = cfl_number / (largest + speed_eps)

    def update(x, carry):
        for k in range(8):
            out[k, x] = m[k, x] - step * acc[x, k]
        return carry

    lax.fori_loop(0, X, update, 0)
    gathered(total, 1)
    both = jnp.sum(total[...], axis=0)
    both = both - step * pltpu.roll(jnp.broadcast_to(both, (8, LANES)), LANES - 8, 1)[0:1]
    tot_ref[...] = both / float(count * X * Y * Z)

    for copy in sent:
        copy.wait_send()

    def drain(offset, carry):
        for which, buffer in ((0, peak), (1, total)):
            spread_copy(buffer, which, offset).wait_send()
        return carry

    lax.fori_loop(1, count, drain, 0)


def shards(sizes, moments, velocity, drift):
    _, X, Y, Z = moments.shape
    count = sizes[0] * sizes[1] * sizes[2]
    f32 = jnp.float32
    vm = lambda *shape: pltpu.VMEM(shape, f32)
    updated, totals = pl.pallas_call(
        functools.partial(kernel, sizes),
        name="transport",
        out_shape=(
            pltpu.VMEM(moments.shape, f32), pltpu.VMEM((1, LANES), f32)
        ),
        in_specs=[pl.BlockSpec(memory_space=pl.ANY)] * 3,
        out_specs=(
            pl.BlockSpec(memory_space=pltpu.VMEM), pl.BlockSpec(memory_space=pltpu.VMEM)
        ),
        scratch_shapes=[
            vm(8, X, Y, Z), vm(3, X, Y, Z), vm(3, X, Y, Z), vm(X + 2, 8, Y, Z), vm(X, 8, Y, Z),
            vm(X + 1, 8, Y, Z), vm(X, 8, Y, Z), vm(X, 8, Y, Z),
            vm(2, 2, Y, Z), vm(2, X, 2, Z), vm(2, X, 2, Z), vm(2, X, Y, LANES),
            vm(2, X, Y, LANES), vm(2, X, 8, Z), vm(2, X, 8, Z), vm(2, X, Y, LANES),
            vm(2, X, Y, LANES), vm(count, 1, LANES), vm(count, 1, LANES),
            pltpu.SemaphoreType.DMA((X + 2,)),
            pltpu.SemaphoreType.DMA((14,)), pltpu.SemaphoreType.DMA((14,)),
            pltpu.SemaphoreType.DMA((2, count)), pltpu.SemaphoreType.DMA((2, count)),
        ],
        compiler_params=pltpu.CompilerParams(collective_id=0, has_side_effects=True),
    )(moments, velocity, drift)
    return updated, totals[0, :8]


def solution(mesh):
    spec = P(None, "gx", "gy", "gz")
    sizes = tuple(mesh.shape[a] for a in AXES)
    return jax.shard_map(
        functools.partial(shards, sizes), mesh=mesh, in_specs=(spec,) * 3,
        out_specs=(spec, P()), check_vma=False,
    )
```

profile of v0, /device:TPU:0, one launch (start us, length us, event | category | flops | bytes accessed | tf_op | source)
XLA Modules:
  0.0 30.0 jit_solution(6262719103450104338)
XLA Ops:
  0.6 27.9 %transport.1 = (f32[8,4,16,512]{3,2,1,0:T(8,128)S(1)}, f32[1,128]{1,0:T(1,128)S(1)}) custom-call(f32[8,4,16,512]{3,2,1,0:T(8,128)} %m_hbm.1, f32[3,4,16,512]{3,2,1,0:T(8,128)} %v_hbm.1, f32[3,4,16,512]{3,2,1,0:T(8,128)} %g_hbm.1), custom_call_target="tpu_custom_call" | custom-call | tf_op jit(solution)/shard_map/transport/pallas_call | solution.py:444
  28.5 1.0 %copy.6 = f32[8,4,16,512]{3,2,1,0:T(8,128)} copy(f32[8,4,16,512]{3,2,1,0:T(8,128)S(1)} %get-tuple-element.6) | data formatting | bytes 2097152
  29.5 0.5 %slice_bitcast_fusion = f32[8]{0:T(128)} fusion(f32[1,128]{1,0:T(1,128)S(1)} %get-tuple-element.5), kind=kLoop, calls=%fused_computation | loop fusion | bytes 64 | tf_op jit(solution)/shard_map/squeeze | solution.py:466
where the time goes:
time: 30.1 us; the launch traced here: 30 us
  Pallas kernels  27.9 us (93%)
  local copies, waits for them, and re-layouts  1.48 us (5%)
  between operations  0.64 us (2%)
    pallas_call x1, Pallas kernels, shards(): pl.pallas_call(functools.partial(kernel, sizes), name='transport', out_sh...  27.9 us
    unnamed x1, local copies, waits for them, and re-layouts  0.97 us

commit v1 on v0

v1 whole, which is shorter than its diff:
```python
import functools

import jax
import jax.numpy as jnp
from jax import lax
from jax.experimental import pallas as pl
from jax.experimental.pallas import tpu as pltpu
from jax.sharding import PartitionSpec as P

SWEEPS = 6
AXES = ("gx", "gy", "gz")
LANES = 128
SUBLANES = 8

cfl_number = 0.4
speed_eps = 1e-06
pair_list = ((0, 1), (0, 2), (0, 3), (1, 2), (1, 3), (2, 3))


def entry_key(i, j):
    return (min(i, j), max(i, j))


def scaled(scale, value):
    return value if scale is None else scale * value


def sheared(alpha, beta, near, far):
    if near is None and far is None:
        return None, None
    if near is None:
        return -(alpha * far), far
    if far is None:
        return near, beta * near
    return near - alpha * far, far + beta * near


def recurrence(moment):
    levels = list(moment)
    before = None
    inverse = 1.0 / levels[0]
    ratios = [levels[1] * inverse]
    alphas = [ratios[0]]
    betas = [levels[0]]
    for level in range(1, 4):
        fresh = [None] * 8
        for column in range(level, 8 - level):
            value = levels[column + 1] - alphas[level - 1] * levels[column]
            if level > 1:
                value = value - betas[level - 1] * before[column]
            fresh[column] = value
        betas.append(fresh[level] * inverse)
        inverse = 1.0 / fresh[level]
        ratios.append(fresh[level + 1] * inverse)
        alphas.append(ratios[level] - ratios[level - 1])
        before, levels = levels, fresh
    return alphas, betas


def invert(moment):
    diag, betas = recurrence(moment)
    table = {(i, j): None for i in range(4) for j in range(i + 1, 4)}
    for i in range(3):
        table[i, i + 1] = 2.0 * jnp.sqrt(betas[i + 1])
    scale = [None] * 4
    first = [1.0, None, None, None]
    for _ in range(SWEEPS):
        for p, q in pair_list:
            entry = table[p, q]
            if entry is None:
                continue
            spread = diag[q] - diag[p]
            left = scaled(scale[p], entry)
            right = scaled(scale[q], entry)
            r = lax.rsqrt(spread * spread + left * right)
            r = jnp.where(spread >= 0, r, -r)
            wide = 1.0 + spread * r
            turn = r / wide
            alpha = right * turn
            beta = left * turn
            shift = 0.5 * (left * alpha)
            half = 0.5 * wide
            scale[p] = scaled(scale[p], half)
            scale[q] = scaled(scale[q], half)
            for rest in range(4):
                if rest not in (p, q):
                    a, b = entry_key(rest, p), entry_key(rest, q)
                    table[a], table[b] = sheared(alpha, beta, table[a], table[b])
            diag[p] = diag[p] - shift
            diag[q] = diag[q] + shift
            table[p, q] = None
            first[p], first[q] = sheared(alpha, beta, first[p], first[q])
    weights = [moment[0] * (scale[i] * (first[i] * first[i])) for i in range(4)]
    return weights, diag


def outflow(weights, sizes, mean_speed, mean_drift, upwind):
    sums = None
    for w, s in zip(weights, sizes):
        term = w * upwind(mean_speed + mean_drift * s, 0.0)
        terms = [term]
        for _ in range(7):
            term = term * s
            terms.append(term)
        sums = terms if sums is None else [a + b for a, b in zip(sums, terms)]
    return sums


def kernel(
    sizes, m_hbm, v_hbm, g_hbm, out, tot_ref,
    m, v, g, nodes, acc, fx, zp, zm, yu, zu,
    hvx, vy_s, vy_r, vz_s, vz_r, y_s, y_r, z_s, z_r, table,
    in_sem, nb_send, nb_recv, all_sem, plane_sem,
):
    X, Y, Z = m.shape[1:]
    count = sizes[0] * sizes[1] * sizes[2]
    zc = Z // LANES
    at = [lax.axis_index(a) for a in AXES]
    me = (at[0] * sizes[1] + at[1]) * sizes[2] + at[2]
    row = lax.broadcasted_iota(jnp.int32, (Y, LANES), 0)
    lane = lax.broadcasted_iota(jnp.int32, (Y, LANES), 1)
    bottom = at[2] == 0
    top = at[2] == sizes[2] - 1

    def along(axis, step):
        return lax.rem(at[axis] + step + sizes[axis], sizes[axis])

    def beside(axis, step):
        place = list(at)
        place[axis] = along(axis, step)
        return tuple(place)

    edge = [0] if X == 1 else [0, X - 1]
    inner = list(range(1, X - 1))
    loads = [pltpu.make_async_copy(m_hbm.at[:, x], m.at[:, x], in_sem.at[x]) for x in range(X)]
    loads_v = pltpu.make_async_copy(v_hbm, v, in_sem.at[X])
    loads_g = pltpu.make_async_copy(g_hbm, g, in_sem.at[X + 1])
    for x in edge:
        loads[x].start()
    loads_v.start()
    loads_g.start()
    for x in inner:
        loads[x].start()

    barrier = pltpu.get_barrier_semaphore()
    xs = [along(0, i) for i in range(sizes[0])]
    zs_ = [along(2, i) for i in range(sizes[2])]
    plane = [
        (xs[i], at[1], zs_[j]) for i in range(sizes[0]) for j in range(sizes[2]) if i or j
    ]
    line = [(at[0], along(1, i), at[2]) for i in range(1, sizes[1])]
    for place in plane + line:
        pl.semaphore_signal(
            barrier, inc=1, device_id=place, device_id_type=pl.DeviceIdType.MESH
        )

    sent = []

    def send(src, dst, axis, step):
        index = len(sent)
        copy = pltpu.make_async_remote_copy(
            src_ref=src, dst_ref=dst, send_sem=nb_send.at[index], recv_sem=nb_recv.at[index],
            device_id=beside(axis, step), device_id_type=pl.DeviceIdType.MESH,
        )
        copy.start()
        sent.append(copy)
        return copy

    def solve(layers):
        weights, places = invert(
            [jnp.concatenate([m[k, x] for x in layers], axis=0) for k in range(8)]
        )
        for n, x in enumerate(layers):
            for i in range(4):
                nodes[x + 1, i] = weights[i][n * Y : (n + 1) * Y]
                nodes[x + 1, 4 + i] = places[i][n * Y : (n + 1) * Y]

    def fastest(x):
        speed = None
        for d in range(3):
            vd, gd = v[d, x], g[d, x]
            parts = [jnp.abs(vd + gd * nodes[x + 1, 4 + i]) for i in range(4)]
            largest = jnp.maximum(
                jnp.maximum(parts[0], parts[1]), jnp.maximum(parts[2], parts[3])
            )
            speed = largest if speed is None else speed + largest
        return speed

    for x in edge:
        loads[x].wait()
    solve(edge)
    loads_v.wait()
    loads_g.wait()
    for x in range(X):
        for part, ref in ((0, v), (1, g)):
            vy_s[0, x, part : part + 1, :] = ref[1, x, Y - 1 : Y, :]
            vy_s[1, x, part : part + 1, :] = ref[1, x, 0:1, :]
        high = [ref[2, x, :, Z - LANES : Z] for ref in (v, g)]
        low = [ref[2, x, :, 0:LANES] for ref in (v, g)]
        vz_s[0, x] = jnp.where(lane == 0, pltpu.roll(high[0], 1, 1), pltpu.roll(high[1], 2, 1))
        vz_s[1, x] = jnp.where(lane == 0, low[0], pltpu.roll(low[1], 1, 1))
    pl.semaphore_wait(barrier, len(plane) + len(line))
    velocity_copies = [
        send(vy_s.at[0], vy_r.at[0], 1, 1),
        send(vy_s.at[1], vy_r.at[1], 1, -1),
        send(vz_s.at[0], vz_r.at[0], 2, 1),
        send(vz_s.at[1], vz_r.at[1], 2, -1),
        send(v.at[0, X - 1], hvx.at[0, 0], 0, 1),
        send(g.at[0, X - 1], hvx.at[0, 1], 0, 1),
        send(v.at[0, 0], hvx.at[1, 0], 0, -1),
        send(g.at[0, 0], hvx.at[1, 1], 0, -1),
    ]
    x_copies = [
        send(nodes.at[1], nodes.at[X + 1], 0, -1),
        send(nodes.at[X], nodes.at[0], 0, 1),
    ]
    for place in line:
        pl.semaphore_signal(
            plane_sem, inc=1, device_id=place, device_id_type=pl.DeviceIdType.MESH
        )

    for x in inner:
        loads[x].wait()
    if inner:
        solve(inner)
    best = functools.reduce(jnp.maximum, [fastest(x) for x in range(X)])

    def fold(value):
        value = functools.reduce(
            jnp.add, [value[i : i + SUBLANES, :] for i in range(0, value.shape[0], SUBLANES)]
        )
        return functools.reduce(
            jnp.add, [value[:, i : i + LANES] for i in range(0, value.shape[1], LANES)]
        )

    def lanes_of(chunk):
        return pl.ds(pl.multiple_of(chunk * LANES, LANES), LANES)

    def nodes_of(layer, zs, ys=slice(None)):
        return (
            [nodes[layer, i, ys, zs] for i in range(4)],
            [nodes[layer, 4 + i, ys, zs] for i in range(4)],
        )

    for copy in velocity_copies[:4]:
        copy.wait_recv()

    def means(x, carry):
        for part, ref in ((0, v), (1, g)):
            here = ref[1, x]
            wide_row = lax.broadcasted_iota(jnp.int32, (Y, Z), 0)
            after = vy_r[1, x, part : part + 1, :]
            ahead = vy_r[0, x, part : part + 1, :]
            yu[x, part] = 0.5 * (
                here + jnp.where(wide_row == Y - 1, after, pltpu.roll(here, Y - 1, 0))
            )
            yu[x, 2 + part] = 0.5 * (
                here + jnp.where(wide_row == 0, ahead, pltpu.roll(here, 1, 0))
            )
            here = ref[2, x]
            after = pltpu.roll(vz_r[1, x], LANES - 1 - part, 1)
            ahead = pltpu.roll(vz_r[0, x], LANES - part, 1) if part else vz_r[0, x]
            up = pltpu.roll(here, Z - 1, 1)
            down = pltpu.roll(here, 1, 1)
            for c in range(zc):
                zs = slice(c * LANES, (c + 1) * LANES)
                u, d = up[:, zs], down[:, zs]
                if c == zc - 1:
                    u = jnp.where(lane == LANES - 1, after, u)
                if c == 0:
                    d = jnp.where(lane == 0, ahead, d)
                zu[x, part, :, zs] = 0.5 * (here[:, zs] + u)
                zu[x, 2 + part, :, zs] = 0.5 * (here[:, zs] + d)
        return carry

    lax.fori_loop(0, X, means, 0)

    def side_y(x, carry):
        last = slice(Y - SUBLANES, Y)
        high = outflow(*nodes_of(x + 1, slice(None), last), yu[x, 0, last], yu[x, 1, last], jnp.maximum)
        begin = slice(0, SUBLANES)
        low = outflow(*nodes_of(x + 1, slice(None), begin), yu[x, 2, begin], yu[x, 3, begin], jnp.minimum)
        for k in range(8):
            y_s[0, x, k : k + 1, :] = high[k][SUBLANES - 1 : SUBLANES, :]
            y_s[1, x, k : k + 1, :] = low[k][0:1, :]
        return carry

    lax.fori_loop(0, X, side_y, 0)
    y_copies = [send(y_s.at[0], y_r.at[0], 1, 1), send(y_s.at[1], y_r.at[1], 1, -1)]

    def side_z(x, carry):
        zs = slice(Z - LANES, Z)
        high = outflow(*nodes_of(x + 1, zs), zu[x, 0, :, zs], zu[x, 1, :, zs], jnp.maximum)
        zs = slice(0, LANES)
        low = outflow(*nodes_of(x + 1, zs), zu[x, 2, :, zs], zu[x, 3, :, zs], jnp.minimum)
        packed_high = jnp.zeros((Y, LANES), jnp.float32)
        packed_low = jnp.zeros((Y, LANES), jnp.float32)
        for k in range(8):
            packed_high = jnp.where(lane == k, pltpu.roll(high[k], k + 1, 1), packed_high)
            packed_low = jnp.where(
                lane == k, pltpu.roll(low[k], k, 1) if k else low[k], packed_low
            )
        z_s[0, x] = jnp.where(top, 0.0, packed_high)
        z_s[1, x] = jnp.where(bottom, 0.0, packed_low)
        return carry

    lax.fori_loop(0, X, side_z, 0)
    z_copies = [send(z_s.at[0], z_r.at[0], 2, 1), send(z_s.at[1], z_r.at[1], 2, -1)]

    for copy in velocity_copies[4:]:
        copy.wait_recv()

    def drift_of(x, zs):
        return v[0, x, :, zs], g[0, x, :, zs]

    def between(left, right):
        return 0.5 * (left[0] + right[0]), 0.5 * (left[1] + right[1])

    def side_x(i, sums):
        zs = lanes_of(i)
        ahead = between((hvx[0, 0, :, zs], hvx[0, 1, :, zs]), drift_of(0, zs))
        after = between(drift_of(X - 1, zs), (hvx[1, 0, :, zs], hvx[1, 1, :, zs]))
        upper = outflow(*nodes_of(X, zs), *after, jnp.maximum)
        lower = outflow(*nodes_of(1, zs), *ahead, jnp.minimum)
        return tuple(a + fold(b) for a, b in zip(sums, upper + lower))

    zero = jnp.zeros((SUBLANES, LANES), jnp.float32)
    x_sums = lax.fori_loop(0, zc, side_x, (zero,) * 16)

    def mass(x, sums):
        return tuple(s + fold(m[k, x]) for k, s in enumerate(sums))

    m_sums = lax.fori_loop(0, X, mass, (zero,) * 8)

    tile_row = lax.broadcasted_iota(jnp.int32, (SUBLANES, LANES), 0)
    tile_lane = lax.broadcasted_iota(jnp.int32, (SUBLANES, LANES), 1)

    def stacked(sums):
        block = zero
        for k in range(8):
            block = jnp.where(tile_row == k, jnp.sum(sums[k], axis=0, keepdims=True), block)
        return block

    blocks = [stacked(m_sums), stacked(x_sums[:8]), stacked(x_sums[8:])]
    for side in range(2):
        part = functools.reduce(jnp.add, [y_s[side, x] for x in range(X)])
        blocks.append(
            functools.reduce(jnp.add, [part[:, i : i + LANES] for i in range(0, Z, LANES)])
        )
    packed = zero
    for n, block in enumerate(blocks):
        value = jnp.sum(block, axis=1, keepdims=True)
        packed = jnp.where(tile_lane == tile_row + 8 * (n + 1), value, packed)
    for side in range(2):
        part = functools.reduce(jnp.add, [z_s[side, x] for x in range(X)])
        part = functools.reduce(
            jnp.add, [part[i : i + SUBLANES] for i in range(0, Y, SUBLANES)]
        )
        packed = packed + pltpu.roll(
            jnp.where(tile_lane < 8, part, 0.0), 8 * (len(blocks) + 1 + side), 1
        )
    packed = jnp.sum(packed, axis=0, keepdims=True)
    best = functools.reduce(
        jnp.maximum,
        [best[i : i + SUBLANES, j : j + LANES]
         for i in range(0, Y, SUBLANES) for j in range(0, Z, LANES)],
    )
    best = jnp.max(jnp.max(best, axis=0, keepdims=True), axis=1, keepdims=True)
    one_lane = lax.broadcasted_iota(jnp.int32, (1, LANES), 1)
    table[me] = jnp.where(one_lane == 0, best, packed)

    pl.semaphore_wait(plane_sem, len(line))

    def spread(j, carry):
        place = jnp.where(j >= me, j + 1, j)
        pltpu.make_async_remote_copy(
            src_ref=table.at[me], dst_ref=table.at[me],
            send_sem=all_sem.at[0], recv_sem=all_sem.at[1],
            device_id=place, device_id_type=pl.DeviceIdType.LOGICAL,
        ).start()
        return carry

    lax.fori_loop(0, count - 1, spread, 0)

    def side_faces(i, carry):
        x, chunk = lax.div(i, zc), lax.rem(i, zc)
        zs = lanes_of(chunk)
        w, s = nodes_of(x + 1, zs)
        high = outflow(w, s, yu[x, 0, :, zs], yu[x, 1, :, zs], jnp.maximum)
        for k in range(8):
            acc[x, k, :, zs] = high[k] - jnp.where(row == 0, 0.0, pltpu.roll(high[k], 1, 0))
        low = outflow(w, s, yu[x, 2, :, zs], yu[x, 3, :, zs], jnp.minimum)
        for k in range(8):
            acc[x, k, :, zs] += (
                jnp.where(row == Y - 1, 0.0, pltpu.roll(low[k], Y - 1, 0)) - low[k]
            )
        return carry

    lax.fori_loop(0, X * zc, side_faces, 0)

    def wall_faces(i, carry):
        x, chunk = lax.div(i, zc), lax.rem(i, zc)
        zs = lanes_of(chunk)
        w, s = nodes_of(x + 1, zs)
        shut_high = (lane == LANES - 1) & ((chunk == zc - 1) & top)
        shut_low = (lane == 0) & ((chunk == 0) & bottom)
        high = outflow(w, s, zu[x, 0, :, zs], zu[x, 1, :, zs], jnp.maximum)
        for k in range(8):
            zp[x, k, :, zs] = jnp.where(shut_high, 0.0, high[k])
        low = outflow(w, s, zu[x, 2, :, zs], zu[x, 3, :, zs], jnp.minimum)
        for k in range(8):
            zm[x, k, :, zs] = jnp.where(shut_low, 0.0, low[k])
        return carry

    lax.fori_loop(0, X * zc, wall_faces, 0)

    def face_x(face, zs, left, right):
        mean = between(left, right)
        upper = outflow(*nodes_of(face, zs), *mean, jnp.maximum)
        lower = outflow(*nodes_of(face + 1, zs), *mean, jnp.minimum)
        for k in range(8):
            fx[face, k, :, zs] = upper[k] + lower[k]

    def inner_x(i, carry):
        face, zs = lax.div(i, zc) + 1, lanes_of(lax.rem(i, zc))
        face_x(face, zs, drift_of(face - 1, zs), drift_of(face, zs))
        return carry

    def outer_x(i, carry):
        zs = lanes_of(i)
        face_x(0, zs, (hvx[0, 0, :, zs], hvx[0, 1, :, zs]), drift_of(0, zs))
        face_x(X, zs, drift_of(X - 1, zs), (hvx[1, 0, :, zs], hvx[1, 1, :, zs]))
        return carry

    if X > 1:
        lax.fori_loop(0, (X - 1) * zc, inner_x, 0)

    for copy in x_copies:
        copy.wait_recv()
    lax.fori_loop(0, zc, outer_x, 0)
    for copy in y_copies + z_copies:
        copy.wait_recv()

    wide_row = lax.broadcasted_iota(jnp.int32, (Y, Z), 0)
    wide_lane = lax.broadcasted_iota(jnp.int32, (Y, Z), 1)

    def combine(x, carry):
        low_all, high_all = z_r[0, x], z_r[1, x]
        for k in range(8):
            fp, fm = zp[x, k], zm[x, k]
            first = pltpu.roll(low_all, LANES - k, 1) if k else low_all
            last = pltpu.roll(high_all, LANES - 1 - k, 1)
            spare = [first] * (zc - 1)
            before = jnp.where(
                wide_lane == 0, jnp.concatenate([first] + spare, 1), pltpu.roll(fp, 1, 1)
            )
            spare = [last] * (zc - 1)
            after = jnp.where(
                wide_lane == Z - 1, jnp.concatenate(spare + [last], 1), pltpu.roll(fm, Z - 1, 1)
            )
            change = acc[x, k] + ((fp + after) - (fm + before))
            change = change + (fx[x + 1, k] - fx[x, k])
            change = change + jnp.where(
                wide_row == Y - 1, y_r[1, x, k : k + 1, :],
                jnp.where(wide_row == 0, -y_r[0, x, k : k + 1, :], 0.0),
            )
            acc[x, k] = change
        return carry

    lax.fori_loop(0, X, combine, 0)

    every = pltpu.make_async_copy(
        table.at[pl.ds(0, count - 1)], table.at[pl.ds(0, count - 1)], all_sem.at[1]
    )
    every.wait()
    rows = table[...]
    largest = jnp.max(jnp.max(rows, axis=0)[:, 0:1], axis=1, keepdims=True)
    step = cfl_number / (largest + speed_eps)

    def update(x, carry):
        for k in range(8):
            out[k, x] = m[k, x] - step * acc[x, k]
        return carry

    lax.fori_loop(0, X, update, 0)

    grid = rows.reshape(sizes + (1, LANES))

    def turned(axis, step):
        size = sizes[axis]
        cut = (size - step) % size
        if cut == 0:
            return grid
        return jnp.concatenate(
            [lax.slice_in_dim(grid, cut, size, axis=axis), lax.slice_in_dim(grid, 0, cut, axis=axis)],
            axis=axis,
        )

    group = one_lane // 8
    net = jnp.zeros((1, LANES), jnp.float32)
    for axis in range(3):
        rise = jnp.sum((grid - turned(axis, 1)).reshape(count, 1, LANES), axis=0)
        fall = jnp.sum((turned(axis, -1) - grid).reshape(count, 1, LANES), axis=0)
        net = net + jnp.where(group == 2 + 2 * axis, rise, jnp.where(group == 3 + 2 * axis, fall, 0.0))
    net = jnp.broadcast_to(net, (SUBLANES, LANES))
    change = functools.reduce(jnp.add, [pltpu.roll(net, LANES - 8 * n, 1) for n in range(2, 8)])[0:1]
    both = pltpu.roll(jnp.broadcast_to(jnp.sum(rows, axis=0), (SUBLANES, LANES)), LANES - 8, 1)[0:1]
    tot_ref[...] = (both - step * change) / float(count * X * Y * Z)

    for copy in sent:
        copy.wait_send()
    pltpu.make_async_copy(
        table.at[pl.ds(0, count - 1)], table.at[pl.ds(0, count - 1)], all_sem.at[0]
    ).wait()


def shards(sizes, moments, velocity, drift):
    _, X, Y, Z = moments.shape
    count = sizes[0] * sizes[1] * sizes[2]
    f32 = jnp.float32
    vm = lambda *shape: pltpu.VMEM(shape, f32)
    updated, totals = pl.pallas_call(
        functools.partial(kernel, sizes),
        name="transport",
        out_shape=(
            pltpu.VMEM(moments.shape, f32), pltpu.VMEM((1, LANES), f32)
        ),
        in_specs=[pl.BlockSpec(memory_space=pl.ANY)] * 3,
        out_specs=(
            pl.BlockSpec(memory_space=pltpu.VMEM), pl.BlockSpec(memory_space=pltpu.VMEM)
        ),
        scratch_shapes=[
            vm(8, X, Y, Z), vm(3, X, Y, Z), vm(3, X, Y, Z), vm(X + 2, 8, Y, Z), vm(X, 8, Y, Z),
            vm(X + 1, 8, Y, Z), vm(X, 8, Y, Z), vm(X, 8, Y, Z), vm(X, 4, Y, Z), vm(X, 4, Y, Z),
            vm(2, 2, Y, Z), vm(2, X, 2, Z), vm(2, X, 2, Z), vm(2, X, Y, LANES),
            vm(2, X, Y, LANES), vm(2, X, 8, Z), vm(2, X, 8, Z), vm(2, X, Y, LANES),
            vm(2, X, Y, LANES), vm(count, 1, LANES),
            pltpu.SemaphoreType.DMA((X + 2,)),
            pltpu.SemaphoreType.DMA((14,)), pltpu.SemaphoreType.DMA((14,)),
            pltpu.SemaphoreType.DMA((2,)), pltpu.SemaphoreType.REGULAR,
        ],
        compiler_params=pltpu.CompilerParams(collective_id=0, has_side_effects=True),
    )(moments, velocity, drift)
    return updated, totals[0, :8]


def solution(mesh):
    spec = P(None, "gx", "gy", "gz")
    sizes = tuple(mesh.shape[a] for a in AXES)
    return jax.shard_map(
        functools.partial(shards, sizes), mesh=mesh, in_specs=(spec,) * 3,
        out_specs=(spec, P()), check_vma=False,
    )
```

time: 30.1 us -> 22.5 us (0.75)
  Pallas kernels: 27.9 us -> 20.3 us
    pallas_call x1, Pallas kernels: 27.9 us -> 20.3 us  [shards(): pl.pallas_call(functools.partial(kernel, sizes), name='transport', out_sh...]
where the time goes in v1:
time: 22.5 us; the launch traced here: 22.4 us
  Pallas kernels  20.3 us (90%)
  local copies, waits for them, and re-layouts  1.48 us (7%)
  between operations  0.64 us (3%)
    pallas_call x1, Pallas kernels, shards(): pl.pallas_call(functools.partial(kernel, sizes), name='transport', out_sh...  20.3 us
    unnamed x1, local copies, waits for them, and re-layouts  0.97 us
    squeeze x1, local copies, waits for them, and re-layouts, shards(): return (updated, totals[0, :8])  0.51 us

profile of v1, /device:TPU:0, one launch (start us, length us, event | category | flops | bytes accessed | tf_op | source)
XLA Modules:
  0.0 22.4 jit_solution(13280729245270495072)
XLA Ops:
  0.6 20.3 %transport.1 = (f32[8,4,16,512]{3,2,1,0:T(8,128)S(1)}, f32[1,128]{1,0:T(1,128)S(1)}) custom-call(f32[8,4,16,512]{3,2,1,0:T(8,128)} %m_hbm.1, f32[3,4,16,512]{3,2,1,0:T(8,128)} %v_hbm.1, f32[3,4,16,512]{3,2,1,0:T(8,128)} %g_hbm.1), custom_call_target="tpu_custom_call" | custom-call | tf_op jit(solution)/shard_map/transport/pallas_call | solution.py:522
  20.9 1.0 %copy.6 = f32[8,4,16,512]{3,2,1,0:T(8,128)} copy(f32[8,4,16,512]{3,2,1,0:T(8,128)S(1)} %get-tuple-element.6) | data formatting | bytes 2097152
  21.9 0.5 %slice_bitcast_fusion = f32[8]{0:T(128)} fusion(f32[1,128]{1,0:T(1,128)S(1)} %get-tuple-element.5), kind=kLoop, calls=%fused_computation | loop fusion | bytes 64 | tf_op jit(solution)/shard_map/squeeze | solution.py:544
